TPU v7x, 128 devices: a whole 4x4x4 slice. The times are simulated.
128 devices in a mesh: tp: 16 (over z, x_hi, core), fs: 8 (over y, x_lo).
Axes of the slice: x: 4 (x_hi: 2, x_lo: 2; x = x_hi * 2 + x_lo), y: 4, z: 4, core: 2. Of those that a mesh axis runs over, the one named last changes fastest.
Arguments:
- tokens: bfloat16 [512, 8192], P(('tp', 'fs')), may hold values from -6 to 6
- gate_weight: bfloat16 [8192, 29568], P('fs', 'tp'), may hold values from -0.0625 to 0.0625
- up_weight: bfloat16 [8192, 29568], P('fs', 'tp'), may hold values from -0.0625 to 0.0625
- down_weight: bfloat16 [29568, 8192], P('tp', 'fs'), may hold values from -0.046875 to 0.046875
Outputs:
- mixed: bfloat16 [512, 8192], P(None, ('fs', 'tp'))
All inputs are finite; a program needn't handle non-finite values.
Results may differ from a plain program's by a relative error of at most 0.0049.
Values may be sent and summed in bfloat16 or wider, within the bound.
No kernel may reach another device: no remote copies, remote signals or barrier semaphores. Data moves between devices by JAX's collectives and lax.ppermute only.
A program may use at most 64 MiB of HBM per device.

v0:
```python
import jax
import jax.numpy as jnp
from jax import lax
from jax.sharding import Mesh
from jax.sharding import PartitionSpec as P

FS = ("fs_0", "fs_1")
TP_FS = ("tp", "fs_0", "fs_1")
FS_TP = ("fs_0", "fs_1", "tp")


def laid_out(pieces, dim):
    dims = list(pieces.shape[1:])
    dims[dim] *= pieces.shape[0]
    return jnp.moveaxis(pieces, 0, dim).reshape(dims)


def copy_for_each(shard, axis):
    copies = jnp.broadcast_to(shard, (lax.axis_size(axis), *shard.shape))
    return lax.all_to_all(copies, axis, split_axis=0, concat_axis=0, tiled=True)


def gather_directly(shard, axis, dim):
    return laid_out(copy_for_each(shard, axis), dim)


def sum_by_axis(shard, axes, dim):
    for axis in axes:
        shard = lax.psum_scatter(shard, axis, scatter_dimension=dim, tiled=True)
    return shard


def cut_along(shard, dim, count):
    before, after = (shard.shape[:dim], shard.shape[dim + 1 :])
    return jnp.moveaxis(shard.reshape(*before, count, -1, *after), dim, 0)


def sent_and_summed(shard, axis, dim):
    pieces = cut_along(shard, dim, lax.axis_size(axis))
    arrived = lax.all_to_all(pieces, axis, split_axis=0, concat_axis=0, tiled=True)
    return arrived.sum(axis=0)


def body(tokens, gate_weight, up_weight, down_weight):
    by_feature = lax.all_to_all(tokens, FS, split_axis=1, concat_axis=0, tiled=True)
    feature_rows = gather_directly(by_feature, "tp", 0)
    gate_part = jnp.dot(feature_rows, gate_weight, preferred_element_type=jnp.float32)
    up_part = jnp.dot(feature_rows, up_weight, preferred_element_type=jnp.float32)
    gate, up = (sum_by_axis(gate_part, FS, 1), sum_by_axis(up_part, FS, 1))
    hidden = (jax.nn.silu(gate) * up).astype(jnp.bfloat16)
    group_hidden = gather_directly(hidden, FS, 1)
    partial_cols = jnp.dot(group_hidden, down_weight, preferred_element_type=jnp.float32)
    summed = sent_and_summed(partial_cols, "tp", 1)
    return summed.astype(jnp.bfloat16)


def solution(mesh):
    finer = Mesh(mesh.devices.reshape(mesh.shape["tp"], 4, 2), ("tp", "fs_0", "fs_1"))
    in_specs = (P(TP_FS, None), P(FS, "tp"), P(FS, "tp"), P("tp", FS))
    out_specs = P(None, FS_TP)
    return jax.shard_map(body, mesh=finer, in_specs=in_specs, out_specs=out_specs, check_vma=False)
```

profile of v0, /device:TPU:1, one launch (start us, length us, event | category | flops | bytes accessed | tf_op | source)
XLA Modules:
  0.0 244.5 jit_solution(6208779732393416822)
XLA Ops:
  0.0 11.1 %all_to_all.34 = bf16[4,8,1024]{2,0,1:T(4,128)(2,1)S(1)} all-to-all(bf16[4,8,1024]{2,0,1:T(4,128)(2,1)} %bitcast.34), channel_id=1, replica_groups=mesh['tp'=16,'fs_0'=4,'fs_1'=2] {'fs_0','fs_1'}, dimensions={1} | all-to-all | bytes 131072 | tf_op jit(solution)/shard_map/all_to_all | solution.py:45
  11.2 0.1 broadcast_in_dim.6
  11.3 26.2 %all_to_all.35 = bf16[16,32,1024]{2,1,0:T(8,128)(2,1)S(1)} all-to-all(bf16[16,32,1024]{2,1,0:T(8,128)(2,1)S(1)} %broadcast_in_dim.6), channel_id=1, replica_groups=mesh['tp'=16,'fs_0'=4,'fs_1'=2] {'tp'}, dimensions={0} | all-to-all | bytes 2097152 | tf_op jit(solution)/shard_map/all_to_all | solution.py:20
  37.5 6.3 %fusion.7 = f32[512,1848]{0,1:T(8,128)} fusion(bf16[512,1024]{1,0:T(8,128)(2,1)S(1)} %bitcast.31, bf16[1024,1848]{0,1:T(8,128)(2,1)} %param.5), kind=kOutput, calls=%fused_computation.5 | convolution fusion | flops 1937768448 | bytes 8617984 | tf_op jit(solution)/shard_map/dot_general | solution.py:47
  43.7 4.1 %fusion.8 = f32[512,1848]{0,1:T(8,128)} fusion(bf16[512,1024]{1,0:T(8,128)(2,1)S(1)} %bitcast.32, bf16[1024,1848]{0,1:T(8,128)(2,1)S(1)} %copy-done.3), kind=kOutput, calls=%fused_computation.6 | convolution fusion | flops 1937768448 | bytes 8617984 | tf_op jit(solution)/shard_map/dot_general | solution.py:48
  47.8 87.6 %fusion.5 = (f32[512,464]{0,1:T(8,128)S(1)}, f32[512,464]{0,1:T(8,128)S(1)}) fusion(f32[512,1848]{0,1:T(8,128)} %fusion.8, f32[512,1848]{0,1:T(8,128)} %fusion.7), kind=kCustom, calls=%all-reduce-scatter.4 | all-reduce-scatter fusion | flops 1900545 | bytes 9470464
  135.4 1.6 collective-permute-start
  137.0 0.6 dynamic-slice.10
  138.3 2.5 %collective-permute-start.2 = (f32[512,6]{0,1:T(8,128)S(1)}, f32[512,6]{0,1:T(8,128)S(1)}, u32[]{:S(2)}, u32[]{:S(2)}) collective-permute-start(f32[512,6]{0,1:T(8,128)S(1)} %slice.2), channel_id=1, source_target_pairs={{0,2},{2,4},{4,6},{1,3},{3,5},{5,7},{8,10},{10,12},{12,14},{9,11},... | collective-permute-start | bytes 36872
  140.8 0.0 collective-permute-done
  140.8 1.3 concatenate
  142.1 1.1 constant_dynamic-slice_fusion.1
  143.2 0.0 collective-permute-done.2
  143.2 1.3 concatenate.2
  144.6 0.1 constant_dynamic-slice_fusion
  144.7 22.0 %fusion.6 = (f32[512,232]{0,1:T(8,128)S(1)}, f32[512,232]{0,1:T(8,128)S(1)}) fusion(f32[512,462]{0,1:T(8,128)S(1)} %constant_dynamic-slice_fusion, f32[512,462]{0,1:T(8,128)S(1)} %copy-done), kind=kCustom, calls=%all-reduce-scatter.5 | all-reduce-scatter fusion | flops 475137 | bytes 2843136
  166.8 2.1 collective-permute-start.1
  168.9 1.3 collective-permute-start.3
  170.2 0.6 dynamic-slice.14
  171.5 0.0 collective-permute-done.1
  171.5 0.4 concatenate.1
  171.8 0.0 collective-permute-done.3
  171.8 0.4 concatenate.3
  172.2 0.2 fusion.4
  172.4 1.4 broadcast_in_dim.7
  173.8 3.6 %all-to-all-start.2 = ((bf16[8,512,231]{1,2,0:T(8,128)(2,1)}), bf16[8,512,231]{1,2,0:T(8,128)(2,1)S(1)}, u32[]{:S(2)}, u32[]{:S(2)}) async-start(bf16[8,512,231]{1,2,0:T(8,128)(2,1)} %broadcast_in_dim.7), calls=%async_computation.2 | async-start | bytes 3801088 | tf_op jit(solution)/shard_map/all_to_all | solution.py:20
  177.4 6.0 %copy.9 = bf16[1848,1024]{0,1:T(8,128)(2,1)} copy(bf16[1848,1024]{1,0:T(8,128)(2,1)} %param.7) | data formatting | bytes 7569408 | tf_op args[3]
  183.4 15.2 %all-to-all-done.2 = bf16[8,512,231]{1,2,0:T(8,128)(2,1)S(1)} async-done(((bf16[8,512,231]{1,2,0:T(8,128)(2,1)}), bf16[8,512,231]{1,2,0:T(8,128)(2,1)S(1)}, u32[]{:S(2)}, u32[]{:S(2)}) %all-to-all-start.2) | async-done | bytes 1892384 | tf_op jit(solution)/shard_map/all_to_all | solution.py:20
  198.6 1.8 reshape.13
  200.5 5.0 %convolution_bitcast_fusion = f32[16,512,64]{1,2,0:T(8,128)S(1)} fusion(bf16[512,1848,1]{0,1,2:T(8,128)(2,1)} %reshape.13, bf16[16,64,1848]{2,1,0:T(8,128)(2,1)} %bitcast.30), kind=kOutput, calls=%fused_computation | convolution fusion | flops 1937768448 | bytes 7774208 | tf_op jit(solution)/shard_map/dot_general | solution.py:52
  205.5 38.2 %all_to_all.36 = f32[16,512,64]{1,2,0:T(8,128)S(1)} all-to-all(f32[16,512,64]{1,2,0:T(8,128)S(1)} %convolution_bitcast_fusion), channel_id=1, replica_groups=mesh['tp'=16,'fs_0'=4,'fs_1'=2] {'tp'}, dimensions={0} | all-to-all | bytes 4194304 | tf_op jit(solution)/shard_map/all_to_all | solution.py:40
  243.7 0.8 reduce_sum.9
  (13 shorter events, 0.1 us)
Async XLA Ops:
  37.4 6.3 %copy-start.3 = (bf16[1024,1848]{0,1:T(8,128)(2,1)S(1)}, bf16[1024,1848]{0,1:T(8,128)(2,1)}, u32[]{:S(2)}) copy-start(bf16[1024,1848]{0,1:T(8,128)(2,1)} %param.6) | copy-start | bytes 11354116
  47.8 89.2 %copy-start.2 = (u32[128]{0:T(128)S(1)}, u32[128]{0:T(128)}, u32[]{:S(2)}) copy-start(u32[128]{0:T(128)} %constant.11) | copy-start | bytes 1540
  135.4 5.3 %collective-permute-start = (f32[512,6]{0,1:T(8,128)S(1)}, f32[512,6]{0,1:T(8,128)S(1)}, u32[]{:S(2)}, u32[]{:S(2)}) collective-permute-start(f32[512,6]{0,1:T(8,128)S(1)} %slice), channel_id=1, source_target_pairs={{0,2},{2,4},{4,6},{1,3},{3,5},{5,7},{8,10},{10,12},{12,14},{9,11},... | collective-permute-start | bytes 36872
  138.3 4.9 %collective-permute-start.2 = (f32[512,6]{0,1:T(8,128)S(1)}, f32[512,6]{0,1:T(8,128)S(1)}, u32[]{:S(2)}, u32[]{:S(2)}) collective-permute-start(f32[512,6]{0,1:T(8,128)S(1)} %slice.2), channel_id=1, source_target_pairs={{0,2},{2,4},{4,6},{1,3},{3,5},{5,7},{8,10},{10,12},{12,14},{9,11},... | collective-permute-start | bytes 36872
  143.2 1.5 copy-start
  143.2 27.0 %copy-start.1 = (u32[128]{0:T(128)S(1)}, u32[128]{0:T(128)}, u32[]{:S(2)}) copy-start(u32[128]{0:T(128)} %constant.15) | copy-start | bytes 1540
  166.8 4.7 %collective-permute-start.1 = (f32[512,1]{0,1:T(1,128)S(1)}, f32[512,1]{0,1:T(1,128)S(1)}, u32[]{:S(2)}, u32[]{:S(2)}) collective-permute-start(f32[512,1]{0,1:T(1,128)S(1)} %slice.1), channel_id=1, source_target_pairs={{0,1},{2,3},{4,5},{6,7},{8,9},{10,11},{12,13},{14,15},{16,17},{18,... | collective-permute-start | bytes 6152
  168.9 2.9 %collective-permute-start.3 = (f32[512,1]{0,1:T(1,128)S(1)}, f32[512,1]{0,1:T(1,128)S(1)}, u32[]{:S(2)}, u32[]{:S(2)}) collective-permute-start(f32[512,1]{0,1:T(1,128)S(1)} %slice.3), channel_id=1, source_target_pairs={{0,1},{2,3},{4,5},{6,7},{8,9},{10,11},{12,13},{14,15},{16,17},{18,... | collective-permute-start | bytes 6152
  173.8 24.9 %all-to-all-start.2 = ((bf16[8,512,231]{1,2,0:T(8,128)(2,1)}), bf16[8,512,231]{1,2,0:T(8,128)(2,1)S(1)}, u32[]{:S(2)}, u32[]{:S(2)}) async-start(bf16[8,512,231]{1,2,0:T(8,128)(2,1)} %broadcast_in_dim.7), calls=%async_computation.2 | async-start | bytes 3801088 | tf_op jit(solution)/shard_map/all_to_all | solution.py:20
where the time goes:
time: 245 us; the launch traced here: 244 us
  blocking collectives  185 us (76%)
  matrix products  15.4 us (6%)
  local copies, waits for them, and re-layouts  15.2 us (6%)
  waiting for transfers between devices  15.2 us (6%)
  starting transfers between devices  11 us (4%)
    unnamed x2, blocking collectives  110 us
    all_to_all x1, blocking collectives, sent_and_summed(): lax.all_to_all(pieces, axis, split_axis=0, concat_axis=0, tiled=True)  38.2 us
    all_to_all x1, blocking collectives, copy_for_each(): return lax.all_to_all(copies, axis, split_axis=0, concat_axis=0, tiled=True)  26.2 us
    all_to_all x1, waiting for transfers between devices, copy_for_each(): return lax.all_to_all(copies, axis, split_axis=0, concat_axis=0, tiled=True)  15.2 us
    unnamed x21, local copies, waits for them, and re-layouts  11.8 us
    all_to_all x1, blocking collectives, body(): lax.all_to_all(tokens, FS, split_axis=1, concat_axis=0, tiled=True)  11.1 us
    unnamed x4, starting transfers between devices  7.45 us
    dot_general x1, matrix products, body(): jnp.dot(feature_rows, gate_weight, preferred_element_type=jnp.float32)  6.28 us
  transfers between devices with their start and end apart: 5, of which 1 were waited for; matrix products, arithmetic and copies ran while one was open for 4% of the time, Pallas kernels for 0%

commit v1 on v0

v1 whole, which is shorter than its diff:
```python
import jax
import jax.numpy as jnp
from jax import lax
from jax.sharding import Mesh
from jax.sharding import PartitionSpec as P

FS = ("y", "xl")
TP = ("z", "xh", "c")
TP_FS = TP + FS
FS_TP = FS + TP
ROWS = 232


def exchanged(pieces, axes):
    return lax.all_to_all(pieces, axes, split_axis=0, concat_axis=0, tiled=True)


def gathered(shard, axes, count):
    copies = jnp.broadcast_to(shard, (count, *shard.shape))
    return exchanged(copies, axes).reshape(-1, *shard.shape[1:])


def units_by_device(part):
    padded = jnp.pad(part.astype(jnp.bfloat16), ((0, 8 * ROWS - part.shape[0]), (0, 0)))
    return padded.reshape(8, ROWS, -1)


def body(tokens, gate_weight, up_weight, down_weight):
    by_feature = lax.all_to_all(tokens, FS, split_axis=1, concat_axis=0, tiled=True)
    rows = gathered(by_feature, TP, 16)
    units = gate_weight.shape[1]
    contract = (((0,), (1,)), ((), ()))
    gate_part = lax.dot_general(gate_weight, rows, contract, preferred_element_type=jnp.float32)
    up_part = lax.dot_general(up_weight, rows, contract, preferred_element_type=jnp.float32)
    parts = jnp.concatenate([units_by_device(gate_part), units_by_device(up_part)], axis=1)
    sums = exchanged(parts, FS).astype(jnp.float32).sum(axis=0)
    gate, up = sums[:ROWS], sums[ROWS:]
    hidden = (jax.nn.silu(gate) * up).astype(jnp.bfloat16)
    group_hidden = gathered(hidden, FS, 8)[:units]
    contract = (((0,), (0,)), ((), ()))
    partial_cols = lax.dot_general(down_weight, group_hidden, contract, preferred_element_type=jnp.float32)
    arrived = exchanged(partial_cols.astype(jnp.bfloat16).reshape(16, 64, -1), TP)
    return arrived.astype(jnp.float32).sum(axis=0).astype(jnp.bfloat16).T


def solution(mesh):
    finer = Mesh(mesh.devices.reshape(4, 2, 2, 4, 2), TP_FS)
    in_specs = (P(TP_FS, None), P(FS, TP), P(FS, TP), P(TP, FS))
    out_specs = P(None, FS_TP)
    return jax.shard_map(body, mesh=finer, in_specs=in_specs, out_specs=out_specs, check_vma=False)
```

time: 245 us -> 146 us (0.60)
  blocking collectives: 185 us -> 134 us
  waiting for transfers between devices: 15.2 us -> 0 us
  local copies, waits for them, and re-layouts: 15.2 us -> 1.06 us
  starting transfers between devices: 11 us -> 0 us
  matrix products: 15.4 us -> 9.01 us
    unnamed x2 -> x0, blocking collectives: 110 us -> none
    all_to_all x2 -> x4, blocking collectives: 64.4 us -> 122 us  [exchanged(): return lax.all_to_all(pieces, axes, split_axis=0, concat_axis=0, tiled=True)]
    all_to_all x1 -> x0, waiting for transfers between devices: 15.2 us -> none  [copy_for_each(): return lax.all_to_all(copies, axis, split_axis=0, concat_axis=0, tiled=True)]
    unnamed x21 -> x4, local copies, waits for them, and re-layouts: 11.8 us -> 0.01 us
    unnamed x4 -> x0, starting transfers between devices: 7.45 us -> none
    dot_general x3, matrix products: 15.4 us -> 9.01 us  [the longest x1 4.39 us: body(): lax.dot_general(up_weight, rows, contract, preferred_element_type=jnp.flo...]
    all_to_all x1 -> x0, starting transfers between devices: 3.59 us -> none  [copy_for_each(): return lax.all_to_all(copies, axis, split_axis=0, concat_axis=0, tiled=True)]
  transfers between devices with their start and end apart: 5 -> 0, of which waited for: 1 -> 0; matrix products, arithmetic and copies ran while one was open for 4% -> 0% of each run, Pallas kernels for 0% -> 0%
where the time goes in v1:
time: 146 us
  blocking collectives  134 us (92%)
  matrix products  9.01 us (6%)
  other arithmetic  1.81 us (1%)
    all_to_all x4, blocking collectives, exchanged(): return lax.all_to_all(pieces, axes, split_axis=0, concat_axis=0, tiled=True)  122 us
    all_to_all x1, blocking collectives, body(): lax.all_to_all(tokens, FS, split_axis=1, concat_axis=0, tiled=True)  11.1 us
    dot_general x1, matrix products, body(): lax.dot_general(up_weight, rows, contract, preferred_element_type=jnp.flo...  4.39 us

profile of v1, /device:TPU:1, one launch (start us, length us, event | category | flops | bytes accessed | tf_op | source)
XLA Modules:
  0.0 145.6 jit_solution(7552358543716943544)
XLA Ops:
  0.0 11.1 %all_to_all.39 = bf16[4,8,1024]{2,0,1:T(4,128)(2,1)S(1)} all-to-all(bf16[4,8,1024]{2,0,1:T(4,128)(2,1)} %bitcast.22), channel_id=1, replica_groups=mesh['z'=4,'xh'=2,'c'=2,'y'=4,'xl'=2] {'y','xl'}, dimensions={1} | all-to-all | bytes 131072 | tf_op jit(solution)/shard_map/all_to_all | solution.py:29
  11.2 0.1 broadcast_in_dim.6
  11.3 26.2 %all_to_all.40 = bf16[16,32,1024]{2,1,0:T(8,128)(2,1)S(1)} all-to-all(bf16[16,32,1024]{2,1,0:T(8,128)(2,1)S(1)} %broadcast_in_dim.6), channel_id=1, replica_groups=mesh['z'=4,'xh'=2,'c'=2,'y'=4,'xl'=2] {'z','xh','c'}, dimensions={0} | all-to-all | bytes 2097152 | tf_op jit(solution)/shard_map/all_to_all | solution.py:15
  37.4 0.0 copy-start
  37.5 4.4 %convolution_convert_fusion = bf16[1848,512]{1,0:T(8,128)(2,1)S(1)} fusion(bf16[1024,1848]{0,1:T(8,128)(2,1)} %param.6, bf16[512,1024]{1,0:T(8,128)(2,1)S(1)} %bitcast.19), kind=kOutput, calls=%fused_computation.2 | convolution fusion | flops 1938714624 | bytes 6725632 | tf_op jit(solution)/shard_map/dot_general | solution.py:34
  41.8 0.0 copy-done
  41.9 2.2 %convolution_convert_fusion.1 = bf16[1848,512]{1,0:T(8,128)(2,1)S(1)} fusion(bf16[1024,1848]{0,1:T(8,128)(2,1)S(1)} %copy-done, bf16[512,1024]{1,0:T(8,128)(2,1)S(1)} %bitcast.20), kind=kOutput, calls=%fused_computation.3 | convolution fusion | flops 1938714624 | bytes 6725632 | tf_op jit(solution)/shard_map/dot_general | solution.py:33
  44.1 0.1 pad.8
  44.2 0.1 pad.7
  44.3 0.4 pad_maximum_fusion
  44.7 46.4 %all_to_all.41 = bf16[8,464,512]{2,1,0:T(8,128)(2,1)S(1)} all-to-all(bf16[8,464,512]{2,1,0:T(8,128)(2,1)S(1)} %pad_maximum_fusion), channel_id=1, replica_groups=mesh['z'=4,'xh'=2,'c'=2,'y'=4,'xl'=2] {'y','xl'}, dimensions={0} | all-to-all | bytes 7602176 | tf_op jit(solution)/shard_map/all_to_all | solution.py:15
  91.1 0.5 convert_reduce_fusion
  91.6 0.0 copy-start.1
  91.6 0.1 fusion.8
  91.8 0.1 broadcast_in_dim.7
  91.9 25.8 %all_to_all.42 = bf16[8,232,512]{2,1,0:T(8,128)(2,1)S(1)} all-to-all(bf16[8,232,512]{2,1,0:T(8,128)(2,1)S(1)} %broadcast_in_dim.7), channel_id=1, replica_groups=mesh['z'=4,'xh'=2,'c'=2,'y'=4,'xl'=2] {'y','xl'}, dimensions={0} | all-to-all | bytes 3801088 | tf_op jit(solution)/shard_map/all_to_all | solution.py:15
  117.7 0.0 copy-done.1
  117.7 2.4 %fusion.5 = bf16[1024,512]{0,1:T(8,128)(2,1)S(1)} fusion(bf16[1848,1024]{1,0:T(8,128)(2,1)S(1)} %copy-done.1, bf16[1856,512]{1,0:T(8,128)(2,1)S(1)} %bitcast.18), kind=kOutput, calls=%fused_computation.7 | convolution fusion | flops 1938292736 | bytes 6725632 | tf_op jit(solution)/shard_map/dot_general | solution.py:41
  120.1 0.5 copy.6
  120.7 24.2 %all_to_all.43 = bf16[16,64,512]{2,1,0:T(8,128)(2,1)S(1)} all-to-all(bf16[16,64,512]{2,1,0:T(8,128)(2,1)S(1)} %bitcast.17), channel_id=1, replica_groups=mesh['z'=4,'xh'=2,'c'=2,'y'=4,'xl'=2] {'z','xh','c'}, dimensions={0} | all-to-all | bytes 2097152 | tf_op jit(solution)/shard_map/all_to_all | solution.py:15
  144.8 0.8 reduce_sum.22
  (1 shorter events, 0.0 us)
Async XLA Ops:
  37.4 4.4 %copy-start = (bf16[1024,1848]{0,1:T(8,128)(2,1)S(1)}, bf16[1024,1848]{0,1:T(8,128)(2,1)}, u32[]{:S(2)}) copy-start(bf16[1024,1848]{0,1:T(8,128)(2,1)} %param.5) | copy-start | bytes 11354116
  91.6 26.1 %copy-start.1 = (bf16[1848,1024]{1,0:T(8,128)(2,1)S(1)}, bf16[1848,1024]{1,0:T(8,128)(2,1)}, u32[]{:S(2)}) copy-start(bf16[1848,1024]{1,0:T(8,128)(2,1)} %param.7) | copy-start | bytes 11354116

commit v2 on v1

v2 whole, which is shorter than its diff:
```python
import functools

import jax
import jax.numpy as jnp
from jax import lax
from jax.experimental import pallas as pl
from jax.experimental.pallas import tpu as pltpu
from jax.sharding import Mesh
from jax.sharding import PartitionSpec as P

FS = ("y", "xl")
TP = ("z", "xh", "c")
TP_FS = TP + FS
FS_TP = FS + TP
FIRST, SECOND = 112, 120
SPLIT = 8 * FIRST
TURNS = (2, 1, 3)
f32, bf16 = jnp.float32, jnp.bfloat16


def at(array, index):
    return lax.dynamic_index_in_dim(array, index, 0, keepdims=False)


def put(buffer, piece, index):
    return lax.dynamic_update_index_in_dim(buffer, piece, index, 0)


def swapped(piece, axis):
    return lax.ppermute(piece, axis, [(0, 1), (1, 0)])


def turned(piece, axis, step):
    return lax.ppermute(piece, axis, [(i, (i + step) % 4) for i in range(4)])


def pair_of(own, other, place):
    both = jnp.zeros((2, *own.shape), own.dtype)
    return put(put(both, own, place), other, 1 - place)


def gathered(own, axis, place):
    pieces = put(jnp.zeros((4, *own.shape), own.dtype), own, place)
    for step in TURNS:
        pieces = put(pieces, turned(own, axis, step), (place - step) % 4)
    return pieces


def activated(sums):
    return (jax.nn.silu(sums[..., 0, :, :]) * sums[..., 1, :, :]).astype(bf16)


def products_kernel(height, where, rows, gate, up, out, held, sems):
    steps, span = held.shape[0], out.shape[2]
    pieces = height // span
    copies = []
    for step in range(steps):
        for kind, weight in enumerate((gate, up)):
            window = weight.at[pl.ds(pl.multiple_of(where[step], 8), height)]
            copies.append(pltpu.make_async_copy(window, held.at[step, kind], sems.at[step, kind]))
            copies[-1].start()
    for step in range(steps):
        for kind in range(2):
            copies[2 * step + kind].wait()
            result = lax.dot_general(held[step, kind], rows[...], (((1,), (1,)), ((), ())), preferred_element_type=f32)
            for piece in range(pieces):
                out[step * pieces + piece, kind] = result[piece * span : (piece + 1) * span].astype(out.dtype)


def products(rows, gate, up, starts, pieces, span, dtype):
    height, (count, depth) = pieces * span, rows.shape
    steps = len(starts)
    vmem, hbm = (pl.BlockSpec(memory_space=space) for space in (pltpu.VMEM, pltpu.HBM))
    flops = 4 * steps * height * count * depth
    return pl.pallas_call(
        functools.partial(products_kernel, height),
        out_shape=jax.ShapeDtypeStruct((steps * pieces, 2, span, count), dtype),
        in_specs=[pl.BlockSpec(memory_space=pltpu.SMEM), vmem, hbm, hbm],
        out_specs=vmem,
        scratch_shapes=[pltpu.VMEM((steps, 2, height, depth), bf16), pltpu.SemaphoreType.DMA((steps, 2))],
        compiler_params=pltpu.CompilerParams(vmem_limit_bytes=14 << 20),
        cost_estimate=pl.CostEstimate(flops=flops, bytes_accessed=4 * steps * height * depth, transcendentals=0),
    )(jnp.stack(starts).astype(jnp.int32), rows, gate, up)


def down_kernel(where, weight, group, own, out):
    core = where[0]
    half = weight.shape[1] // 2
    for part in range(2):
        block = weight[:, part * half : (part + 1) * half]
        result = lax.dot_general(block, group[...], (((0,), (0,)), ((), ())), preferred_element_type=f32)
        for i in range(4):
            low, high = result[128 * i : 128 * i + 64], result[128 * i + 64 : 128 * (i + 1)]
            own[4 * part + i] = jnp.where(core == 0, low, high)
            out[4 * part + i] = jnp.where(core == 0, high, low)


def down_products(weight, group, core):
    (units, columns), count = weight.shape, group.shape[1]
    vmem = pl.BlockSpec(memory_space=pltpu.VMEM)
    shape = jax.ShapeDtypeStruct((8, columns // 16, count), f32)
    return pl.pallas_call(
        down_kernel,
        out_shape=(shape, shape),
        in_specs=[pl.BlockSpec(memory_space=pltpu.SMEM), vmem, vmem],
        out_specs=(vmem, vmem),
        compiler_params=pltpu.CompilerParams(vmem_limit_bytes=20 << 20),
        cost_estimate=pl.CostEstimate(flops=2 * units * columns * count, bytes_accessed=2 * units * columns, transcendentals=0),
        name="down",
    )(jnp.reshape(core, (1,)).astype(jnp.int32), weight, group)


def body(tokens, gate_weight, up_weight, down_weight):
    z, xh, c, y, xl = (lax.axis_index(name) for name in TP_FS)
    units = gate_weight.shape[1]
    gate, up = (pltpu.with_memory_space_constraint(w.T, pltpu.HBM) for w in (gate_weight, up_weight))

    by_feature = lax.all_to_all(tokens, FS, split_axis=1, concat_axis=0, tiled=True)
    line = pair_of(by_feature, swapped(by_feature, "xh"), xh)
    plane = gathered(line, "z", z).reshape(8, 1, *by_feature.shape)
    rows = jnp.zeros((8, 2, *by_feature.shape), bf16)
    rows = lax.dynamic_update_slice(rows, plane, (0, c, 0, 0))
    rows = lax.dynamic_update_slice(rows, swapped(plane, "c"), (0, 1 - c, 0, 0))
    rows = rows.reshape(512, -1)

    def second_starts(half):
        start = SPLIT + half * (units - SPLIT - 4 * SECOND)
        return [start, start + 2 * SECOND]

    def first_start(turn):
        return (y + turn) % 4 * (2 * FIRST)

    q_out = products(rows, gate, up, second_starts(1 - xl), 2, SECOND, bf16)
    q_got = swapped(q_out, "xl")
    p_out = products(rows, gate, up, [first_start(turn) for turn in TURNS], 2, FIRST, bf16)
    p_got = [turned(p_out[2 * i : 2 * i + 2], "y", turn) for i, turn in enumerate(TURNS)]
    q_own = products(rows, gate, up, second_starts(xl), 2, SECOND, f32)
    p_own = products(rows, gate, up, [first_start(0)], 2, FIRST, f32)

    def q_sum(turn):
        place = (y + turn) % 4
        return at(q_own, place) + at(q_got, place).astype(f32)

    def q_send(turn):
        return q_sum(turn).astype(bf16)

    q_arrived = [turned(q_send(turn), "y", turn).astype(f32) for turn in TURNS]
    p_sum = p_own + sum(piece.astype(f32) for piece in p_got)
    p_arrived = swapped(at(p_sum, 1 - xl).astype(bf16), "xl").astype(f32)
    p_hidden = activated(at(p_sum, xl) + p_arrived)
    q_hidden = activated(q_sum(0) + sum(q_arrived))

    def placed(group, piece, row):
        return lax.dynamic_update_slice(group, piece, (row, 0))

    def p_row(y_at, xl_at):
        return (y_at * 2 + xl_at) * FIRST

    def q_row(y_at, xl_at):
        return SPLIT + xl_at * (units - SPLIT - 4 * SECOND) + y_at * SECOND

    p_column = gathered(p_hidden, "y", y)
    q_other = swapped(q_hidden, "xl")
    q_pair = jnp.stack([q_hidden, q_other])
    group = placed(jnp.zeros((units, 512), bf16), q_hidden, q_row(y, xl))
    group = placed(group, q_other, q_row(y, 1 - xl))
    p_other = swapped(p_column, "xl")
    for place in range(4):
        group = placed(group, p_column[place], p_row(place, xl))
        group = placed(group, p_other[place], p_row(place, 1 - xl))
    for turn in TURNS:
        arrived, place = turned(q_pair, "y", turn), (y - turn) % 4
        group = placed(group, arrived[0], q_row(place, xl))
        group = placed(group, arrived[1], q_row(place, 1 - xl))

    own_part, out_part = down_products(down_weight, group, c)
    sums = (own_part + swapped(out_part, "c")).reshape(4, 2, 64, -1)
    z_sum = at(sums, z)
    for turn in TURNS:
        z_sum += turned(at(sums, (z + turn) % 4).astype(bf16), "z", turn).astype(f32)
    total = at(z_sum, xh) + swapped(at(z_sum, 1 - xh).astype(bf16), "xh").astype(f32)
    return total.astype(bf16).T


def solution(mesh):
    finer = Mesh(mesh.devices.reshape(4, 2, 2, 4, 2), TP_FS)
    in_specs = (P(TP_FS, None), P(FS, TP), P(FS, TP), P(TP, FS))
    out_specs = P(None, FS_TP)
    return jax.shard_map(body, mesh=finer, in_specs=in_specs, out_specs=out_specs, check_vma=False)
```

time: 146 us -> 145 us (level)
  blocking collectives: 134 us -> 0 us
  waiting for transfers between devices: 0 us -> 82.1 us
  starting transfers between devices: 0 us -> 41.8 us
  Pallas kernels: 0 us -> 15.9 us
  matrix products: 9.01 us -> 0 us
    all_to_all x5 -> x0, blocking collectives: 134 us -> none  [the longest x4 122 us: exchanged(): return lax.all_to_all(pieces, axes, split_axis=0, concat_axis=0, tiled=True)]
    ppermute x0 -> x26, waiting for transfers between devices: none -> 76.9 us  [the longest x18 51.2 us: turned(): return lax.ppermute(piece, axis, [(i, (i + step) % 4) for i in range(4)])]
    ppermute x0 -> x26, starting transfers between devices: none -> 35.8 us  [the longest x18 24.7 us: turned(): return lax.ppermute(piece, axis, [(i, (i + step) % 4) for i in range(4)])]
    pallas_call x0 -> x5, Pallas kernels: none -> 15.9 us  [the longest x4 13.5 us: products(): pl.pallas_call(functools.partial(products_kernel, height), out_shape=jax....]
    dot_general x3 -> x0, matrix products: 9.01 us -> none  [the longest x1 4.39 us: body(): lax.dot_general(up_weight, rows, contract, preferred_element_type=jnp.flo...]
    all_to_all x0 -> x1, starting transfers between devices: none -> 5.94 us  [body(): lax.all_to_all(tokens, FS, split_axis=1, concat_axis=0, tiled=True)]
    all_to_all x0 -> x1, waiting for transfers between devices: none -> 5.2 us  [body(): lax.all_to_all(tokens, FS, split_axis=1, concat_axis=0, tiled=True)]
  transfers between devices with their start and end apart: 0 -> 27, of which waited for: 0 -> 17; matrix products, arithmetic and copies ran while one was open for 0% -> 1% of each run, Pallas kernels for 0% -> 6%
where the time goes in v2:
time: 145 us; the launch traced here: 144 us
  waiting for transfers between devices  82.1 us (57%)
  starting transfers between devices  41.8 us (29%)
  Pallas kernels  15.9 us (11%)
  other arithmetic  2.16 us (1%)
  local copies, waits for them, and re-layouts  1.82 us (1%)
    ppermute x18, waiting for transfers between devices, turned(): return lax.ppermute(piece, axis, [(i, (i + step) % 4) for i in range(4)])  51.2 us
    ppermute x8, waiting for transfers between devices, swapped(): return lax.ppermute(piece, axis, [(0, 1), (1, 0)])  25.7 us
    ppermute x18, starting transfers between devices, turned(): return lax.ppermute(piece, axis, [(i, (i + step) % 4) for i in range(4)])  24.7 us
    pallas_call x4, Pallas kernels, products(): pl.pallas_call(functools.partial(products_kernel, height), out_shape=jax....  13.5 us
    ppermute x8, starting transfers between devices, swapped(): return lax.ppermute(piece, axis, [(0, 1), (1, 0)])  11.1 us
    all_to_all x1, starting transfers between devices, body(): lax.all_to_all(tokens, FS, split_axis=1, concat_axis=0, tiled=True)  5.94 us
    all_to_all x1, waiting for transfers between devices, body(): lax.all_to_all(tokens, FS, split_axis=1, concat_axis=0, tiled=True)  5.2 us
  transfers between devices with their start and end apart: 27, of which 17 were waited for; matrix products, arithmetic and copies ran while one was open for 1% of the time, Pallas kernels for 6%

profile of v2, /device:TPU:1, one launch (start us, length us, event | category | flops | bytes accessed | tf_op | source)
XLA Modules:
  0.0 144.1 jit_solution(7972341544125591478)
XLA Ops:
  0.0 5.9 %all-to-all-start = ((bf16[4,8,1024]{2,0,1:T(4,128)(2,1)}), bf16[4,8,1024]{2,0,1:T(4,128)(2,1)S(1)}, u32[]{:S(2)}, u32[]{:S(2)}) async-start(bf16[4,8,1024]{2,0,1:T(4,128)(2,1)} %bitcast.178), calls=%async_computation | async-start | bytes 131072 | tf_op jit(solution)/shard_map/all_to_all | solution.py:118
  5.9 5.2 %all-to-all-done = bf16[4,8,1024]{2,0,1:T(4,128)(2,1)S(1)} async-done(((bf16[4,8,1024]{2,0,1:T(4,128)(2,1)}), bf16[4,8,1024]{2,0,1:T(4,128)(2,1)S(1)}, u32[]{:S(2)}, u32[]{:S(2)}) %all-to-all-start) | async-done | bytes 65568 | tf_op jit(solution)/shard_map/all_to_all | solution.py:118
  11.2 2.5 %collective-permute-start = (bf16[32,1024]{1,0:T(8,128)(2,1)S(1)}, bf16[32,1024]{1,0:T(8,128)(2,1)S(1)}, u32[]{:S(2)}, u32[]{:S(2)}) collective-permute-start(bf16[32,1024]{1,0:T(8,128)(2,1)S(1)} %all_to_all.17), channel_id=1, source_target_pairs={{0,16},{16,0},{1,17},{17,1},{2,18},{18,2},{3,19},{19,3},{4,20},{20... | collective-permute-start | bytes 196616 | tf_op jit(solution)/shard_map/ppermute | solution.py:30
  13.7 2.1 %collective-permute-done = bf16[32,1024]{1,0:T(8,128)(2,1)S(1)} collective-permute-done((bf16[32,1024]{1,0:T(8,128)(2,1)S(1)}, bf16[32,1024]{1,0:T(8,128)(2,1)S(1)}, u32[]{:S(2)}, u32[]{:S(2)}) %collective-permute-start) | collective-permute-done | bytes 65568 | tf_op jit(solution)/shard_map/ppermute | solution.py:30
  15.9 3.7 %collective-permute-start.1 = (bf16[2,32,1024]{2,1,0:T(8,128)(2,1)S(1)}, bf16[2,32,1024]{2,1,0:T(8,128)(2,1)S(1)}, u32[]{:S(2)}, u32[]{:S(2)}) collective-permute-start(bf16[2,32,1024]{2,1,0:T(8,128)(2,1)S(1)} %bitcast_dynamic-update-slice_fusion.7), channel_id=1, source_target_pairs={{0,64},{32,96},{64,0},{96,32},{1,65},{33,97},{65,1},{97,33},{2,66}... | collective-permute-start | bytes 393224 | tf_op jit(solution)/shard_map/ppermute | solution.py:34
  20.3 1.9 %collective-permute-start.3 = (bf16[2,32,1024]{2,1,0:T(8,128)(2,1)S(1)}, bf16[2,32,1024]{2,1,0:T(8,128)(2,1)S(1)}, u32[]{:S(2)}, u32[]{:S(2)}) collective-permute-start(bf16[2,32,1024]{2,1,0:T(8,128)(2,1)S(1)} %bitcast_dynamic-update-slice_fusion.7), channel_id=1, source_target_pairs={{0,96},{32,0},{64,32},{96,64},{1,97},{33,1},{65,33},{97,65},{2,98}... | collective-permute-start | bytes 393224 | tf_op jit(solution)/shard_map/ppermute | solution.py:34
  22.4 3.6 %collective-permute-done.2 = bf16[2,32,1024]{2,1,0:T(8,128)(2,1)S(1)} collective-permute-done((bf16[2,32,1024]{2,1,0:T(8,128)(2,1)S(1)}, bf16[2,32,1024]{2,1,0:T(8,128)(2,1)S(1)}, u32[]{:S(2)}, u32[]{:S(2)}) %collective-permute-start.2) | collective-permute-done | bytes 131104 | tf_op jit(solution)/shard_map/ppermute | solution.py:34
  26.1 3.4 %collective-permute-start.4 = (bf16[8,1,32,1024]{3,2,1,0:T(8,128)(2,1)S(1)}, bf16[8,1,32,1024]{3,2,1,0:T(8,128)(2,1)S(1)}, u32[]{:S(2)}, u32[]{:S(2)}) collective-permute-start(bf16[8,1,32,1024]{3,2,1,0:T(8,128)(2,1)S(1)} %bitcast.173), channel_id=1, source_target_pairs={{0,8},{8,0},{1,9},{9,1},{2,10},{10,2},{3,11},{11,3},{4,12},{12,4},... | collective-permute-start | bytes 1572872 | tf_op jit(solution)/shard_map/ppermute | solution.py:30
  31.0 4.5 %shard_map.49 = bf16[6,2,112,512]{3,2,1,0:T(8,128)(2,1)S(1)} custom-call(s32[3]{0:T(128)S(1)} %pad_add_fusion.2.where, bf16[512,1024]{1,0:T(8,128)(2,1)S(1)} %bitcast.159, bf16[1848,1024]{1,0:T(8,128)(2,1)} %bitcast.163, bf16[1848,1024]{1,0:T(8,128)(2,1)} %bitcast.167), custom_call_target="tpu_custom_call" | custom-call | flops 1409286144 | bytes 2752512 | tf_op jit(solution)/shard_map/pallas_call | solution.py:75
  37.9 2.2 %collective-permute-start.12 = (bf16[2,2,112,512]{3,2,1,0:T(8,128)(2,1)S(1)}, bf16[2,2,112,512]{3,2,1,0:T(8,128)(2,1)S(1)}, u32[]{:S(2)}, u32[]{:S(2)}) collective-permute-start(bf16[2,2,112,512]{3,2,1,0:T(8,128)(2,1)S(1)} %get-tuple-element.15), channel_id=1, source_target_pairs={{0,6},{2,0},{4,2},{6,4},{1,7},{3,1},{5,3},{7,5},{8,14},{10,8},{12,... | collective-permute-start | bytes 1376264 | tf_op jit(solution)/shard_map/ppermute | solution.py:34
  40.2 2.0 %shard_map.48 = f32[2,2,112,512]{3,2,1,0:T(8,128)S(1)} custom-call(s32[1]{0:T(128)} %bitcast.22.where, bf16[512,1024]{1,0:T(8,128)(2,1)S(1)} %bitcast.160, bf16[1848,1024]{1,0:T(8,128)(2,1)} %bitcast.164, bf16[1848,1024]{1,0:T(8,128)(2,1)} %bitcast.168), custom_call_target="tpu_custom_call" | custom-call | flops 469762048 | bytes 917504 | tf_op jit(solution)/shard_map/pallas_call | solution.py:75
  42.2 7.7 %collective-permute-done.10 = bf16[2,2,112,512]{3,2,1,0:T(8,128)(2,1)S(1)} collective-permute-done((bf16[2,2,112,512]{3,2,1,0:T(8,128)(2,1)}, bf16[2,2,112,512]{3,2,1,0:T(8,128)(2,1)S(1)}, u32[]{:S(2)}, u32[]{:S(2)}) %collective-permute-start.10) | collective-permute-done | bytes 458784 | tf_op jit(solution)/shard_map/ppermute | solution.py:34
  49.9 10.5 %collective-permute-done.11 = bf16[2,2,112,512]{3,2,1,0:T(8,128)(2,1)S(1)} collective-permute-done((bf16[2,2,112,512]{3,2,1,0:T(8,128)(2,1)S(1)}, bf16[2,2,112,512]{3,2,1,0:T(8,128)(2,1)S(1)}, u32[]{:S(2)}, u32[]{:S(2)}) %collective-permute-start.11) | collective-permute-done | bytes 458784 | tf_op jit(solution)/shard_map/ppermute | solution.py:34
  61.3 3.5 %shard_map.47 = bf16[4,2,120,512]{3,2,1,0:T(8,128)(2,1)S(1)} custom-call(s32[2]{0:T(128)S(1)} %pad_add_fusion.1.where, bf16[512,1024]{1,0:T(8,128)(2,1)S(1)} %bitcast.161, bf16[1848,1024]{1,0:T(8,128)(2,1)} %bitcast.165, bf16[1848,1024]{1,0:T(8,128)(2,1)} %bitcast.169), custom_call_target="tpu_custom_call" | custom-call | flops 1006632960 | bytes 1966080 | tf_op jit(solution)/shard_map/pallas_call | solution.py:75
  65.9 3.5 %shard_map.46 = f32[4,2,120,512]{3,2,1,0:T(8,128)S(1)} custom-call(s32[2]{0:T(128)S(1)} %pad_add_fusion.where, bf16[512,1024]{1,0:T(8,128)(2,1)S(1)} %bitcast.162, bf16[1848,1024]{1,0:T(8,128)(2,1)} %bitcast.166, bf16[1848,1024]{1,0:T(8,128)(2,1)} %bitcast.170), custom_call_target="tpu_custom_call" | custom-call | flops 1006632960 | bytes 1966080 | tf_op jit(solution)/shard_map/pallas_call | solution.py:75
  71.1 2.2 %collective-permute-start.16 = (bf16[112,512]{1,0:T(8,128)(2,1)S(1)}, bf16[112,512]{1,0:T(8,128)(2,1)S(1)}, u32[]{:S(2)}, u32[]{:S(2)}) collective-permute-start(bf16[112,512]{1,0:T(8,128)(2,1)S(1)} %fusion.10), channel_id=1, source_target_pairs={{0,6},{2,0},{4,2},{6,4},{1,7},{3,1},{5,3},{7,5},{8,14},{10,8},{12,... | collective-permute-start | bytes 344072 | tf_op jit(solution)/shard_map/ppermute | solution.py:34
  73.4 1.4 %collective-permute-done.14 = bf16[112,512]{1,0:T(8,128)(2,1)S(1)} collective-permute-done((bf16[112,512]{1,0:T(8,128)(2,1)S(1)}, bf16[112,512]{1,0:T(8,128)(2,1)S(1)}, u32[]{:S(2)}, u32[]{:S(2)}) %collective-permute-start.14) | collective-permute-done | bytes 114720 | tf_op jit(solution)/shard_map/ppermute | solution.py:34
  74.9 13.8 %collective-permute-done.5 = bf16[4,2,120,512]{3,2,1,0:T(8,128)(2,1)S(1)} collective-permute-done((bf16[4,2,120,512]{3,2,1,0:T(8,128)(2,1)S(1)}, bf16[4,2,120,512]{3,2,1,0:T(8,128)(2,1)S(1)}, u32[]{:S(2)}, u32[]{:S(2)}) %collective-permute-start.5) | collective-permute-done | bytes 983072 | tf_op jit(solution)/shard_map/ppermute | solution.py:30
  90.5 2.0 %collective-permute-start.8 = (bf16[2,120,512]{2,1,0:T(8,128)(2,1)S(1)}, bf16[2,120,512]{2,1,0:T(8,128)(2,1)S(1)}, u32[]{:S(2)}, u32[]{:S(2)}) collective-permute-start(bf16[2,120,512]{2,1,0:T(8,128)(2,1)S(1)} %get-tuple-element.12), channel_id=1, source_target_pairs={{0,6},{2,0},{4,2},{6,4},{1,7},{3,1},{5,3},{7,5},{8,14},{10,8},{12,... | collective-permute-start | bytes 737288 | tf_op jit(solution)/shard_map/ppermute | solution.py:34
  92.7 4.2 %collective-permute-done.6 = bf16[2,120,512]{2,1,0:T(8,128)(2,1)S(1)} collective-permute-done((bf16[2,120,512]{2,1,0:T(8,128)(2,1)S(1)}, bf16[2,120,512]{2,1,0:T(8,128)(2,1)S(1)}, u32[]{:S(2)}, u32[]{:S(2)}) %collective-permute-start.6) | collective-permute-done | bytes 245792 | tf_op jit(solution)/shard_map/ppermute | solution.py:34
  96.9 6.8 %collective-permute-done.7 = bf16[2,120,512]{2,1,0:T(8,128)(2,1)S(1)} collective-permute-done((bf16[2,120,512]{2,1,0:T(8,128)(2,1)S(1)}, bf16[2,120,512]{2,1,0:T(8,128)(2,1)S(1)}, u32[]{:S(2)}, u32[]{:S(2)}) %collective-permute-start.7) | collective-permute-done | bytes 245792 | tf_op jit(solution)/shard_map/ppermute | solution.py:34
  104.5 4.0 %collective-permute-done.9 = bf16[120,512]{1,0:T(8,128)(2,1)S(1)} collective-permute-done((bf16[120,512]{1,0:T(8,128)(2,1)S(1)}, bf16[120,512]{1,0:T(8,128)(2,1)S(1)}, u32[]{:S(2)}, u32[]{:S(2)}) %collective-permute-start.9) | collective-permute-done | bytes 122912 | tf_op jit(solution)/shard_map/ppermute | solution.py:30
  109.4 2.7 %collective-permute-start.20 = (bf16[2,120,512]{2,1,0:T(8,128)(2,1)S(1)}, bf16[2,120,512]{2,1,0:T(8,128)(2,1)S(1)}, u32[]{:S(2)}, u32[]{:S(2)}) collective-permute-start(bf16[2,120,512]{2,1,0:T(8,128)(2,1)S(1)} %pad_maximum_fusion), channel_id=1, source_target_pairs={{0,6},{2,0},{4,2},{6,4},{1,7},{3,1},{5,3},{7,5},{8,14},{10,8},{12,... | collective-permute-start | bytes 737288 | tf_op jit(solution)/shard_map/ppermute | solution.py:34
  112.3 4.1 %collective-permute-done.18 = bf16[2,120,512]{2,1,0:T(8,128)(2,1)S(1)} collective-permute-done((bf16[2,120,512]{2,1,0:T(8,128)(2,1)S(1)}, bf16[2,120,512]{2,1,0:T(8,128)(2,1)S(1)}, u32[]{:S(2)}, u32[]{:S(2)}) %collective-permute-start.18) | collective-permute-done | bytes 245792 | tf_op jit(solution)/shard_map/ppermute | solution.py:34
  116.4 6.9 %collective-permute-done.19 = bf16[2,120,512]{2,1,0:T(8,128)(2,1)S(1)} collective-permute-done((bf16[2,120,512]{2,1,0:T(8,128)(2,1)S(1)}, bf16[2,120,512]{2,1,0:T(8,128)(2,1)S(1)}, u32[]{:S(2)}, u32[]{:S(2)}) %collective-permute-start.19) | collective-permute-done | bytes 245792 | tf_op jit(solution)/shard_map/ppermute | solution.py:34
  123.4 2.4 %down.1 = (f32[8,64,512]{2,1,0:T(8,128)S(1)}, f32[8,64,512]{2,1,0:T(8,128)S(1)}) custom-call(s32[1]{0:T(128)} %bitcast.where, bf16[1848,1024]{1,0:T(8,128)(2,1)S(1)} %copy-done, bf16[1848,512]{1,0:T(8,128)(2,1)S(1)} %fusion.18.group), custom_call_target="tpu_custom_call" | custom-call | flops 1937768448 | bytes 3784704 | tf_op jit(solution)/shard_map/down/pallas_call | solution.py:102
  126.3 2.3 %collective-permute-done.21 = f32[8,64,512]{2,1,0:T(8,128)S(1)} collective-permute-done((f32[8,64,512]{2,1,0:T(8,128)S(1)}, f32[8,64,512]{2,1,0:T(8,128)S(1)}, u32[]{:S(2)}, u32[]{:S(2)}) %collective-permute-start.21) | collective-permute-done | bytes 1048608 | tf_op jit(solution)/shard_map/ppermute | solution.py:30
  130.1 2.4 %collective-permute-start.23 = (bf16[2,64,512]{2,1,0:T(8,128)(2,1)S(1)}, bf16[2,64,512]{2,1,0:T(8,128)(2,1)S(1)}, u32[]{:S(2)}, u32[]{:S(2)}) collective-permute-start(bf16[2,64,512]{2,1,0:T(8,128)(2,1)S(1)} %get-tuple-element.19), channel_id=1, source_target_pairs={{0,32},{32,64},{64,96},{96,0},{1,33},{33,65},{65,97},{97,1},{2,34}... | collective-permute-start | bytes 393224 | tf_op jit(solution)/shard_map/ppermute | solution.py:34
  132.8 2.4 %collective-permute-done.22 = bf16[2,64,512]{2,1,0:T(8,128)(2,1)S(1)} collective-permute-done((bf16[2,64,512]{2,1,0:T(8,128)(2,1)S(1)}, bf16[2,64,512]{2,1,0:T(8,128)(2,1)S(1)}, u32[]{:S(2)}, u32[]{:S(2)}) %collective-permute-start.22) | collective-permute-done | bytes 131104 | tf_op jit(solution)/shard_map/ppermute | solution.py:34
  135.2 3.5 %collective-permute-done.23 = bf16[2,64,512]{2,1,0:T(8,128)(2,1)S(1)} collective-permute-done((bf16[2,64,512]{2,1,0:T(8,128)(2,1)S(1)}, bf16[2,64,512]{2,1,0:T(8,128)(2,1)S(1)}, u32[]{:S(2)}, u32[]{:S(2)}) %collective-permute-start.23) | collective-permute-done | bytes 131104 | tf_op jit(solution)/shard_map/ppermute | solution.py:34
  138.8 2.5 %collective-permute-start.25 = (bf16[64,512]{1,0:T(8,128)(2,1)S(1)}, bf16[64,512]{1,0:T(8,128)(2,1)S(1)}, u32[]{:S(2)}, u32[]{:S(2)}) collective-permute-start(bf16[64,512]{1,0:T(8,128)(2,1)S(1)} %fusion.33), channel_id=1, source_target_pairs={{0,16},{16,0},{1,17},{17,1},{2,18},{18,2},{3,19},{19,3},{4,20},{20... | collective-permute-start | bytes 196616 | tf_op jit(solution)/shard_map/ppermute | solution.py:30
  141.3 2.2 %collective-permute-done.25 = bf16[64,512]{1,0:T(8,128)(2,1)S(1)} collective-permute-done((bf16[64,512]{1,0:T(8,128)(2,1)S(1)}, bf16[64,512]{1,0:T(8,128)(2,1)S(1)}, u32[]{:S(2)}, u32[]{:S(2)}) %collective-permute-start.25) | collective-permute-done | bytes 65568 | tf_op jit(solution)/shard_map/ppermute | solution.py:30
  (81 shorter events, 15.6 us)
Async XLA Ops:
  0.0 11.1 %all-to-all-start = ((bf16[4,8,1024]{2,0,1:T(4,128)(2,1)}), bf16[4,8,1024]{2,0,1:T(4,128)(2,1)S(1)}, u32[]{:S(2)}, u32[]{:S(2)}) async-start(bf16[4,8,1024]{2,0,1:T(4,128)(2,1)} %bitcast.178), calls=%async_computation | async-start | bytes 131072 | tf_op jit(solution)/shard_map/all_to_all | solution.py:118
  11.2 4.7 %collective-permute-start = (bf16[32,1024]{1,0:T(8,128)(2,1)S(1)}, bf16[32,1024]{1,0:T(8,128)(2,1)S(1)}, u32[]{:S(2)}, u32[]{:S(2)}) collective-permute-start(bf16[32,1024]{1,0:T(8,128)(2,1)S(1)} %all_to_all.17), channel_id=1, source_target_pairs={{0,16},{16,0},{1,17},{17,1},{2,18},{18,2},{3,19},{19,3},{4,20},{20... | collective-permute-start | bytes 196616 | tf_op jit(solution)/shard_map/ppermute | solution.py:30
  15.9 6.4 %collective-permute-start.1 = (bf16[2,32,1024]{2,1,0:T(8,128)(2,1)S(1)}, bf16[2,32,1024]{2,1,0:T(8,128)(2,1)S(1)}, u32[]{:S(2)}, u32[]{:S(2)}) collective-permute-start(bf16[2,32,1024]{2,1,0:T(8,128)(2,1)S(1)} %bitcast_dynamic-update-slice_fusion.7), channel_id=1, source_target_pairs={{0,64},{32,96},{64,0},{96,32},{1,65},{33,97},{65,1},{97,33},{2,66}... | collective-permute-start | bytes 393224 | tf_op jit(solution)/shard_map/ppermute | solution.py:34
  19.6 6.4 %collective-permute-start.2 = (bf16[2,32,1024]{2,1,0:T(8,128)(2,1)S(1)}, bf16[2,32,1024]{2,1,0:T(8,128)(2,1)S(1)}, u32[]{:S(2)}, u32[]{:S(2)}) collective-permute-start(bf16[2,32,1024]{2,1,0:T(8,128)(2,1)S(1)} %bitcast_dynamic-update-slice_fusion.7), channel_id=1, source_target_pairs={{0,32},{32,64},{64,96},{96,0},{1,33},{33,65},{65,97},{97,1},{2,34}... | collective-permute-start | bytes 393224 | tf_op jit(solution)/shard_map/ppermute | solution.py:34
  20.3 5.7 %collective-permute-start.3 = (bf16[2,32,1024]{2,1,0:T(8,128)(2,1)S(1)}, bf16[2,32,1024]{2,1,0:T(8,128)(2,1)S(1)}, u32[]{:S(2)}, u32[]{:S(2)}) collective-permute-start(bf16[2,32,1024]{2,1,0:T(8,128)(2,1)S(1)} %bitcast_dynamic-update-slice_fusion.7), channel_id=1, source_target_pairs={{0,96},{32,0},{64,32},{96,64},{1,97},{33,1},{65,33},{97,65},{2,98}... | collective-permute-start | bytes 393224 | tf_op jit(solution)/shard_map/ppermute | solution.py:34
  26.1 4.9 %collective-permute-start.4 = (bf16[8,1,32,1024]{3,2,1,0:T(8,128)(2,1)S(1)}, bf16[8,1,32,1024]{3,2,1,0:T(8,128)(2,1)S(1)}, u32[]{:S(2)}, u32[]{:S(2)}) collective-permute-start(bf16[8,1,32,1024]{3,2,1,0:T(8,128)(2,1)S(1)} %bitcast.173), channel_id=1, source_target_pairs={{0,8},{8,0},{1,9},{9,1},{2,10},{10,2},{3,11},{11,3},{4,12},{12,4},... | collective-permute-start | bytes 1572872 | tf_op jit(solution)/shard_map/ppermute | solution.py:30
  36.4 13.5 %collective-permute-start.10 = (bf16[2,2,112,512]{3,2,1,0:T(8,128)(2,1)}, bf16[2,2,112,512]{3,2,1,0:T(8,128)(2,1)S(1)}, u32[]{:S(2)}, u32[]{:S(2)}) collective-permute-start(bf16[2,2,112,512]{3,2,1,0:T(8,128)(2,1)} %get-tuple-element.14), channel_id=1, source_target_pairs={{0,4},{2,6},{4,0},{6,2},{1,5},{3,7},{5,1},{7,3},{8,12},{10,14},{12... | collective-permute-start | bytes 1376264 | tf_op jit(solution)/shard_map/ppermute | solution.py:34
  37.4 23.0 %collective-permute-start.11 = (bf16[2,2,112,512]{3,2,1,0:T(8,128)(2,1)S(1)}, bf16[2,2,112,512]{3,2,1,0:T(8,128)(2,1)S(1)}, u32[]{:S(2)}, u32[]{:S(2)}) collective-permute-start(bf16[2,2,112,512]{3,2,1,0:T(8,128)(2,1)S(1)} %get-tuple-element.16), channel_id=1, source_target_pairs={{0,2},{2,4},{4,6},{6,0},{1,3},{3,5},{5,7},{7,1},{8,10},{10,12},{12... | collective-permute-start | bytes 1376264 | tf_op jit(solution)/shard_map/ppermute | solution.py:34
  37.9 22.5 %collective-permute-start.12 = (bf16[2,2,112,512]{3,2,1,0:T(8,128)(2,1)S(1)}, bf16[2,2,112,512]{3,2,1,0:T(8,128)(2,1)S(1)}, u32[]{:S(2)}, u32[]{:S(2)}) collective-permute-start(bf16[2,2,112,512]{3,2,1,0:T(8,128)(2,1)S(1)} %get-tuple-element.15), channel_id=1, source_target_pairs={{0,6},{2,0},{4,2},{6,4},{1,7},{3,1},{5,3},{7,5},{8,14},{10,8},{12,... | collective-permute-start | bytes 1376264 | tf_op jit(solution)/shard_map/ppermute | solution.py:34
  60.7 8.7 %collective-permute-start.13 = (bf16[2,112,512]{2,1,0:T(8,128)(2,1)S(1)}, bf16[2,112,512]{2,1,0:T(8,128)(2,1)S(1)}, u32[]{:S(2)}, u32[]{:S(2)}) collective-permute-start(bf16[2,112,512]{2,1,0:T(8,128)(2,1)S(1)} %fusion.9), channel_id=1, source_target_pairs={{0,1},{1,0},{2,3},{3,2},{4,5},{5,4},{6,7},{7,6},{8,9},{9,8},{10,11... | collective-permute-start | bytes 688136 | tf_op jit(solution)/shard_map/ppermute | solution.py:30
  64.8 23.9 %collective-permute-start.5 = (bf16[4,2,120,512]{3,2,1,0:T(8,128)(2,1)S(1)}, bf16[4,2,120,512]{3,2,1,0:T(8,128)(2,1)S(1)}, u32[]{:S(2)}, u32[]{:S(2)}) collective-permute-start(bf16[4,2,120,512]{3,2,1,0:T(8,128)(2,1)S(1)} %shard_map.47), channel_id=1, source_target_pairs={{0,1},{1,0},{2,3},{3,2},{4,5},{5,4},{6,7},{7,6},{8,9},{9,8},{10,11... | collective-permute-start | bytes 2949128 | tf_op jit(solution)/shard_map/ppermute | solution.py:30
  69.6 5.3 %collective-permute-start.14 = (bf16[112,512]{1,0:T(8,128)(2,1)S(1)}, bf16[112,512]{1,0:T(8,128)(2,1)S(1)}, u32[]{:S(2)}, u32[]{:S(2)}) collective-permute-start(bf16[112,512]{1,0:T(8,128)(2,1)S(1)} %fusion.10), channel_id=1, source_target_pairs={{0,4},{2,6},{4,0},{6,2},{1,5},{3,7},{5,1},{7,3},{8,12},{10,14},{12... | collective-permute-start | bytes 344072 | tf_op jit(solution)/shard_map/ppermute | solution.py:34
  70.6 21.9 %collective-permute-start.15 = (bf16[112,512]{1,0:T(8,128)(2,1)S(1)}, bf16[112,512]{1,0:T(8,128)(2,1)S(1)}, u32[]{:S(2)}, u32[]{:S(2)}) collective-permute-start(bf16[112,512]{1,0:T(8,128)(2,1)S(1)} %fusion.10), channel_id=1, source_target_pairs={{0,2},{2,4},{4,6},{6,0},{1,3},{3,5},{5,7},{7,1},{8,10},{10,12},{12... | collective-permute-start | bytes 344072 | tf_op jit(solution)/shard_map/ppermute | solution.py:34
  71.1 21.4 %collective-permute-start.16 = (bf16[112,512]{1,0:T(8,128)(2,1)S(1)}, bf16[112,512]{1,0:T(8,128)(2,1)S(1)}, u32[]{:S(2)}, u32[]{:S(2)}) collective-permute-start(bf16[112,512]{1,0:T(8,128)(2,1)S(1)} %fusion.10), channel_id=1, source_target_pairs={{0,6},{2,0},{4,2},{6,4},{1,7},{3,1},{5,3},{7,5},{8,14},{10,8},{12,... | collective-permute-start | bytes 344072 | tf_op jit(solution)/shard_map/ppermute | solution.py:34
  88.9 7.9 %collective-permute-start.6 = (bf16[2,120,512]{2,1,0:T(8,128)(2,1)S(1)}, bf16[2,120,512]{2,1,0:T(8,128)(2,1)S(1)}, u32[]{:S(2)}, u32[]{:S(2)}) collective-permute-start(bf16[2,120,512]{2,1,0:T(8,128)(2,1)S(1)} %get-tuple-element.11), channel_id=1, source_target_pairs={{0,4},{2,6},{4,0},{6,2},{1,5},{3,7},{5,1},{7,3},{8,12},{10,14},{12... | collective-permute-start | bytes 737288 | tf_op jit(solution)/shard_map/ppermute | solution.py:34
  89.8 13.8 %collective-permute-start.7 = (bf16[2,120,512]{2,1,0:T(8,128)(2,1)S(1)}, bf16[2,120,512]{2,1,0:T(8,128)(2,1)S(1)}, u32[]{:S(2)}, u32[]{:S(2)}) collective-permute-start(bf16[2,120,512]{2,1,0:T(8,128)(2,1)S(1)} %get-tuple-element.13), channel_id=1, source_target_pairs={{0,2},{2,4},{4,6},{6,0},{1,3},{3,5},{5,7},{7,1},{8,10},{10,12},{12... | collective-permute-start | bytes 737288 | tf_op jit(solution)/shard_map/ppermute | solution.py:34
  90.5 13.2 %collective-permute-start.8 = (bf16[2,120,512]{2,1,0:T(8,128)(2,1)S(1)}, bf16[2,120,512]{2,1,0:T(8,128)(2,1)S(1)}, u32[]{:S(2)}, u32[]{:S(2)}) collective-permute-start(bf16[2,120,512]{2,1,0:T(8,128)(2,1)S(1)} %get-tuple-element.12), channel_id=1, source_target_pairs={{0,6},{2,0},{4,2},{6,4},{1,7},{3,1},{5,3},{7,5},{8,14},{10,8},{12,... | collective-permute-start | bytes 737288 | tf_op jit(solution)/shard_map/ppermute | solution.py:34
  92.6 19.5 %collective-permute-start.17 = (bf16[4,112,512]{2,1,0:T(8,128)(2,1)S(1)}, bf16[4,112,512]{2,1,0:T(8,128)(2,1)S(1)}, u32[]{:S(2)}, u32[]{:S(2)}) collective-permute-start(bf16[4,112,512]{2,1,0:T(8,128)(2,1)S(1)} %bitcast_dynamic-update-slice_fusion.4), channel_id=1, source_target_pairs={{0,1},{1,0},{2,3},{3,2},{4,5},{5,4},{6,7},{7,6},{8,9},{9,8},{10,11... | collective-permute-start | bytes 1376264 | tf_op jit(solution)/shard_map/ppermute | solution.py:30
  104.0 4.5 %collective-permute-start.9 = (bf16[120,512]{1,0:T(8,128)(2,1)S(1)}, bf16[120,512]{1,0:T(8,128)(2,1)S(1)}, u32[]{:S(2)}, u32[]{:S(2)}) collective-permute-start(bf16[120,512]{1,0:T(8,128)(2,1)S(1)} %get-tuple-element.10), channel_id=1, source_target_pairs={{0,1},{1,0},{2,3},{3,2},{4,5},{5,4},{6,7},{7,6},{8,9},{9,8},{10,11... | collective-permute-start | bytes 368648 | tf_op jit(solution)/shard_map/ppermute | solution.py:30
  108.5 14.9 %copy-start = (bf16[1848,1024]{1,0:T(8,128)(2,1)S(1)}, bf16[1848,1024]{1,0:T(8,128)(2,1)}, u32[]{:S(2)}) copy-start(bf16[1848,1024]{1,0:T(8,128)(2,1)} %weight.1) | copy-start | bytes 11354116
  108.5 7.8 %collective-permute-start.18 = (bf16[2,120,512]{2,1,0:T(8,128)(2,1)S(1)}, bf16[2,120,512]{2,1,0:T(8,128)(2,1)S(1)}, u32[]{:S(2)}, u32[]{:S(2)}) collective-permute-start(bf16[2,120,512]{2,1,0:T(8,128)(2,1)S(1)} %pad_maximum_fusion), channel_id=1, source_target_pairs={{0,4},{2,6},{4,0},{6,2},{1,5},{3,7},{5,1},{7,3},{8,12},{10,14},{12... | collective-permute-start | bytes 737288 | tf_op jit(solution)/shard_map/ppermute | solution.py:34
  109.4 13.9 %collective-permute-start.19 = (bf16[2,120,512]{2,1,0:T(8,128)(2,1)S(1)}, bf16[2,120,512]{2,1,0:T(8,128)(2,1)S(1)}, u32[]{:S(2)}, u32[]{:S(2)}) collective-permute-start(bf16[2,120,512]{2,1,0:T(8,128)(2,1)S(1)} %pad_maximum_fusion), channel_id=1, source_target_pairs={{0,2},{2,4},{4,6},{6,0},{1,3},{3,5},{5,7},{7,1},{8,10},{10,12},{12... | collective-permute-start | bytes 737288 | tf_op jit(solution)/shard_map/ppermute | solution.py:34
  109.4 13.9 %collective-permute-start.20 = (bf16[2,120,512]{2,1,0:T(8,128)(2,1)S(1)}, bf16[2,120,512]{2,1,0:T(8,128)(2,1)S(1)}, u32[]{:S(2)}, u32[]{:S(2)}) collective-permute-start(bf16[2,120,512]{2,1,0:T(8,128)(2,1)S(1)} %pad_maximum_fusion), channel_id=1, source_target_pairs={{0,6},{2,0},{4,2},{6,4},{1,7},{3,1},{5,3},{7,5},{8,14},{10,8},{12,... | collective-permute-start | bytes 737288 | tf_op jit(solution)/shard_map/ppermute | solution.py:34
  125.7 2.9 %collective-permute-start.21 = (f32[8,64,512]{2,1,0:T(8,128)S(1)}, f32[8,64,512]{2,1,0:T(8,128)S(1)}, u32[]{:S(2)}, u32[]{:S(2)}) collective-permute-start(f32[8,64,512]{2,1,0:T(8,128)S(1)} %get-tuple-element.8), channel_id=1, source_target_pairs={{0,8},{8,0},{1,9},{9,1},{2,10},{10,2},{3,11},{11,3},{4,12},{12,4},... | collective-permute-start | bytes 3145736 | tf_op jit(solution)/shard_map/ppermute | solution.py:30
  128.9 6.3 %collective-permute-start.22 = (bf16[2,64,512]{2,1,0:T(8,128)(2,1)S(1)}, bf16[2,64,512]{2,1,0:T(8,128)(2,1)S(1)}, u32[]{:S(2)}, u32[]{:S(2)}) collective-permute-start(bf16[2,64,512]{2,1,0:T(8,128)(2,1)S(1)} %get-tuple-element.17), channel_id=1, source_target_pairs={{0,64},{32,96},{64,0},{96,32},{1,65},{33,97},{65,1},{97,33},{2,66}... | collective-permute-start | bytes 393224 | tf_op jit(solution)/shard_map/ppermute | solution.py:34
  130.1 8.6 %collective-permute-start.23 = (bf16[2,64,512]{2,1,0:T(8,128)(2,1)S(1)}, bf16[2,64,512]{2,1,0:T(8,128)(2,1)S(1)}, u32[]{:S(2)}, u32[]{:S(2)}) collective-permute-start(bf16[2,64,512]{2,1,0:T(8,128)(2,1)S(1)} %get-tuple-element.19), channel_id=1, source_target_pairs={{0,32},{32,64},{64,96},{96,0},{1,33},{33,65},{65,97},{97,1},{2,34}... | collective-permute-start | bytes 393224 | tf_op jit(solution)/shard_map/ppermute | solution.py:34
  132.5 6.2 %collective-permute-start.24 = (bf16[2,64,512]{2,1,0:T(8,128)(2,1)S(1)}, bf16[2,64,512]{2,1,0:T(8,128)(2,1)S(1)}, u32[]{:S(2)}, u32[]{:S(2)}) collective-permute-start(bf16[2,64,512]{2,1,0:T(8,128)(2,1)S(1)} %get-tuple-element.18), channel_id=1, source_target_pairs={{0,96},{32,0},{64,32},{96,64},{1,97},{33,1},{65,33},{97,65},{2,98}... | collective-permute-start | bytes 393224 | tf_op jit(solution)/shard_map/ppermute | solution.py:34
  138.8 4.7 %collective-permute-start.25 = (bf16[64,512]{1,0:T(8,128)(2,1)S(1)}, bf16[64,512]{1,0:T(8,128)(2,1)S(1)}, u32[]{:S(2)}, u32[]{:S(2)}) collective-permute-start(bf16[64,512]{1,0:T(8,128)(2,1)S(1)} %fusion.33), channel_id=1, source_target_pairs={{0,16},{16,0},{1,17},{17,1},{2,18},{18,2},{3,19},{19,3},{4,20},{20... | collective-permute-start | bytes 196616 | tf_op jit(solution)/shard_map/ppermute | solution.py:30
